TPU v7x, 32 devices: a whole 2x2x4 slice. The times are simulated.
32 devices in a mesh: row: 2 (over y), col: 4 (over z), depth: 4 (over x, core).
Axes of the slice: x: 2, y: 2, z: 4, core: 2. Of those that a mesh axis runs over, the one named last changes fastest.
Arguments:
- grad_out: bfloat16 [1024, 6144], P('depth', 'col'), may hold values from -6 to 6
- pre_act: bfloat16 [1024, 24576], P('depth', 'row'), may hold values from -8 to 8
- down_weight: bfloat16 [24576, 6144], P(('row', 'depth'), 'col'), may hold values from -0.0546875 to 0.0546875
Outputs:
- grad_pre: bfloat16 [1024, 24576], P('depth', 'row')
- grad_weight: bfloat16 [24576, 6144], P(('row', 'depth'), 'col')
All inputs are finite; a program needn't handle non-finite values.
Results may differ from a plain program's by a relative error of at most 0.0066.
Values may be sent and summed in bfloat16 or wider, within the bound.
A program may use at most 128 MiB of HBM per device.

v0:
```python
import jax
import jax.numpy as jnp
from jax import lax
from jax.sharding import PartitionSpec as P

sqrt_two_pi = 0.7978845608028654
cubic_coeff = 0.044715


def gelu_value(preact):
    tangent = jnp.tanh(sqrt_two_pi * (preact + cubic_coeff * preact * preact * preact))
    return 0.5 * preact * (1.0 + tangent)


def gelu_slope(preact):
    tangent = jnp.tanh(sqrt_two_pi * (preact + cubic_coeff * preact * preact * preact))
    inner = sqrt_two_pi * (1.0 + 3.0 * cubic_coeff * preact * preact)
    return 0.5 * (1.0 + tangent) + 0.5 * preact * (1.0 - tangent * tangent) * inner


def contract_last(left, right):
    return lax.dot_general(
        left, right, (((1,), (1,)), ((), ())), preferred_element_type=jnp.float32
    )


def contract_first(left, right):
    return lax.dot_general(
        left, right, (((0,), (0,)), ((), ())), preferred_element_type=jnp.float32
    )


def finish_rows(partial_value, preacts):
    total = lax.psum(partial_value, "col")
    return (total * gelu_slope(preacts.astype(jnp.float32))).astype(jnp.bfloat16)


def on_device(grad_out, pre_act, down_weight):
    every_grad = lax.all_gather(grad_out, "depth", axis=0, tiled=True)
    own_pre = lax.all_to_all(pre_act, "depth", split_axis=1, concat_axis=0, tiled=True)
    partial_value = contract_last(every_grad, down_weight)
    local_grad = finish_rows(partial_value, own_pre)
    grad_pre = lax.all_to_all(local_grad, "depth", split_axis=0, concat_axis=1, tiled=True)
    own_act = gelu_value(own_pre.astype(jnp.float32)).astype(jnp.bfloat16)
    grad_weight = contract_first(own_act, every_grad).astype(jnp.bfloat16)
    return (grad_pre, grad_weight)


def solution(mesh):
    placed = (P("depth", "col"), P("depth", "row"), P(("row", "depth"), "col"))
    return jax.shard_map(
        on_device,
        mesh=mesh,
        in_specs=placed,
        out_specs=(P("depth", "row"), P(("row", "depth"), "col")),
        check_vma=False,
    )
```

profile of v0, /device:TPU:0, one launch (start us, length us, event | category | flops | bytes accessed | tf_op | source)
XLA Modules:
  0.0 588.5 jit_solution(14912220487641829081)
XLA Ops:
  7.2 0.0 all-gather.2.cloned.1.call-start
  7.2 0.7 all-gather.2.cloned.1.call-update
  7.9 0.0 all-reduce.2.cloned.1.call-start
  7.9 32.8 %all-gather.2.cloned.1.call-done = bf16[1024,1536]{1,0:T(8,128)(2,1)} async-done(((bf16[256,1536]{1,0:T(8,128)(2,1)}), bf16[1024,1536]{1,0:T(8,128)(2,1)}) %all-gather.2.cloned.1.call-update) | async-done | bytes 3145744 | tf_op jit(solution)/shard_map/all_gather | solution.py:39
  40.8 16.2 %fusion.11 = f32[1024,3072]{1,0:T(8,128)} fusion(bf16[1024,1536]{1,0:T(8,128)(2,1)} %all-gather.2.cloned.1.call-done, bf16[3072,1536]{1,0:T(8,128)(2,1)} %param.5), kind=kOutput, calls=%fused_computation.16 | convolution fusion | flops 9663676416 | bytes 25165824 | tf_op jit(solution)/shard_map/dot_general | solution.py:22
  57.0 0.0 all-reduce.2.cloned.1.call-update
  57.0 3.2 copy.10
  60.2 74.3 %all_to_all.32 = bf16[256,4,3072]{2,0,1:T(8,128)(2,1)} all-to-all(bf16[256,4,3072]{2,0,1:T(8,128)(2,1)S(1)} %bitcast.30), channel_id=1, replica_groups=mesh['row'=2,'col'=4,'depth'=4] {'depth'}, dimensions={1} | all-to-all | bytes 12582912 | tf_op jit(solution)/shard_map/all_to_all | solution.py:40
  134.5 348.8 %all-reduce.2.cloned.1.call-done = f32[1024,3072]{1,0:T(8,128)} async-done(((f32[1024,3072]{1,0:T(8,128)}), f32[1024,3072]{1,0:T(8,128)}) %all-reduce.2.cloned.1.call-update) | async-done | bytes 12582928 | tf_op jit(solution)/shard_map/psum | solution.py:34
  483.3 16.1 %fusion.10 = (bf16[1024,3072]{1,0:T(8,128)(2,1)}, bf16[1024,3072]{1,0:T(8,128)(2,1)}) fusion(bf16[256,4,3072]{2,0,1:T(8,128)(2,1)} %all_to_all.32, f32[1024,3072]{1,0:T(8,128)} %all-reduce.2.cloned.1.call-done), kind=kLoop, calls=%fused_computation.13 | loop fusion | flops 69206016 | bytes 31457280 | tf_op jit(solution)/shard_map/convert_element_type | solution.py:44
  499.4 0.0 copy-start
  499.4 5.5 all-to-all-start.1
  504.9 0.0 copy-done
  504.9 14.9 %convolution_convert_fusion = bf16[3072,1536]{1,0:T(8,128)(2,1)} fusion(bf16[1024,3072]{1,0:T(8,128)(2,1)} %get-tuple-element.2, bf16[1024,1536]{1,0:T(8,128)(2,1)S(1)} %copy-done), kind=kOutput, calls=%fused_computation.14 | convolution fusion | flops 9668395008 | bytes 18874368 | tf_op jit(solution)/shard_map/dot_general | solution.py:28
  519.8 55.7 %all-to-all-done.1 = bf16[4,256,3072]{2,1,0:T(8,128)(2,1)} async-done(((bf16[4,256,3072]{2,1,0:T(8,128)(2,1)}), bf16[4,256,3072]{2,1,0:T(8,128)(2,1)}, u32[]{:S(2)}, u32[]{:S(2)}) %all-to-all-start.1) | async-done | bytes 6291488 | tf_op jit(solution)/shard_map/all_to_all | solution.py:43
  575.6 6.1 %copy.8 = bf16[4,32,8,3072]{3,2,0,1:T(8,128)(2,1)} copy(bf16[4,32,8,3072]{3,2,1,0:T(8,128)(2,1)} %bitcast.7) | data formatting | bytes 12582912 | tf_op jit(solution)/shard_map/all_to_all | solution.py:43
Async XLA Ops:
  7.2 33.6 %all-gather.2.cloned.1.call-start = ((), (), s32[]{:S(2)}) async-start(), calls=%async_computation.2 | async-start | bytes 3932160 | tf_op jit(solution)/shard_map/all_gather | solution.py:39
  7.9 475.4 %all-reduce.2.cloned.1.call-start = ((), (), s32[]{:S(2)}) async-start(), calls=%async_computation.3 | async-start | bytes 25165824 | tf_op jit(solution)/shard_map/psum | solution.py:34
  499.4 5.5 copy-start
  499.4 76.2 %all-to-all-start.1 = ((bf16[4,256,3072]{2,1,0:T(8,128)(2,1)}), bf16[4,256,3072]{2,1,0:T(8,128)(2,1)}, u32[]{:S(2)}, u32[]{:S(2)}) async-start(bf16[4,256,3072]{2,1,0:T(8,128)(2,1)} %bitcast.31), calls=%async_computation.1 | async-start | bytes 12582912 | tf_op jit(solution)/shard_map/all_to_all | solution.py:43
Sparse Core Ops, SparseCore 0:
  9.5 31.2 all-gather.1
  57.1 426.1 all-reduce.1
where the time goes:
time: 589 us
  waiting for transfers between devices  438 us (74%)
  blocking collectives  74.3 us (13%)
  matrix products  31.1 us (5%)
  other arithmetic  16.1 us (3%)
  between operations  14.1 us (2%)
  local copies, waits for them, and re-layouts  9.36 us (2%)
    psum x1, waiting for transfers between devices, finish_rows(): total = lax.psum(partial_value, 'col')  349 us
    all_to_all x1, blocking collectives, on_device(): lax.all_to_all(pre_act, 'depth', split_axis=1, concat_axis=0, tiled=True)  74.3 us
    all_to_all x1, waiting for transfers between devices, on_device(): lax.all_to_all(local_grad, 'depth', split_axis=0, concat_axis=1, tiled=True)  55.7 us
    all_gather x1, waiting for transfers between devices, on_device(): every_grad = lax.all_gather(grad_out, 'depth', axis=0, tiled=True)  32.8 us
    dot_general x1, matrix products, contract_last(): lax.dot_general(left, right, (((1,), (1,)), ((), ())), preferred_element_...  16.2 us
    convert_element_type x1, other arithmetic, on_device(): own_act = gelu_value(own_pre.astype(jnp.float32)).astype(jnp.bfloat16)  16.1 us
    dot_general x1, matrix products, contract_first(): lax.dot_general(left, right, (((0,), (0,)), ((), ())), preferred_element_...  14.9 us
  transfers between devices with their start and end apart: 3, of which 3 were waited for; matrix products, arithmetic and copies ran while one was open for 3% of the time, Pallas kernels for 0%

commit v1 on v0

--- a/solution.py
+++ b/solution.py
@@ -31,7 +31,7 @@
 
 
 def finish_rows(partial_value, preacts):
-    total = lax.psum(partial_value, "col")
+    total = jnp.sum(lax.all_gather(partial_value, "col"), axis=0)
     return (total * gelu_slope(preacts.astype(jnp.float32))).astype(jnp.bfloat16)
 
 

time: 589 us -> 1030 us (1.75)
  waiting for transfers between devices: 438 us -> 898 us
  blocking collectives: 74.3 us -> 0 us
  other arithmetic: 16.1 us -> 43.3 us
  local copies, waits for them, and re-layouts: 9.36 us -> 35.9 us
    all_gather x0 -> x1, waiting for transfers between devices: none -> 812 us  [finish_rows(): total = jnp.sum(lax.all_gather(partial_value, 'col'), axis=0)]
    psum x1 -> x0, waiting for transfers between devices: 349 us -> none  [finish_rows(): total = lax.psum(partial_value, 'col')]
    all_to_all x1 -> x0, blocking collectives: 74.3 us -> none  [on_device(): lax.all_to_all(pre_act, 'depth', split_axis=1, concat_axis=0, tiled=True)]
    reduce_sum x0 -> x1, other arithmetic: none -> 23.9 us  [finish_rows(): total = jnp.sum(lax.all_gather(partial_value, 'col'), axis=0)]
    unnamed x2 -> x4, local copies, waits for them, and re-layouts: 0.01 us -> 17.4 us
    convert_element_type x0 -> x1, other arithmetic: none -> 13.3 us  [finish_rows(): (total * gelu_slope(preacts.astype(jnp.float32))).astype(jnp.bfloat16)]
  transfers between devices with their start and end apart: 3 -> 4, of which waited for: 3 -> 3; matrix products, arithmetic and copies ran while one was open for 3% -> 6% of each run, Pallas kernels for 0% -> 0%
where the time goes in v1:
time: 1030 us
  waiting for transfers between devices  898 us (87%)
  other arithmetic  43.3 us (4%)
  local copies, waits for them, and re-layouts  35.9 us (3%)
  matrix products  28.3 us (3%)
  between operations  14.1 us (1%)
  starting transfers between devices  11.3 us (1%)
    all_gather x1, waiting for transfers between devices, finish_rows(): total = jnp.sum(lax.all_gather(partial_value, 'col'), axis=0)  812 us
    all_to_all x1, waiting for transfers between devices, on_device(): lax.all_to_all(local_grad, 'depth', split_axis=0, concat_axis=1, tiled=True)  52.3 us
    all_gather x1, waiting for transfers between devices, on_device(): every_grad = lax.all_gather(grad_out, 'depth', axis=0, tiled=True)  32.8 us
    reduce_sum x1, other arithmetic, finish_rows(): total = jnp.sum(lax.all_gather(partial_value, 'col'), axis=0)  23.9 us
  transfers between devices with their start and end apart: 4, of which 3 were waited for; matrix products, arithmetic and copies ran while one was open for 6% of the time, Pallas kernels for 0%

profile of v1, /device:TPU:0, one launch (start us, length us, event | category | flops | bytes accessed | tf_op | source)
XLA Modules:
  0.0 1030.7 jit_solution(17031740556547483806)
XLA Ops:
  7.2 0.0 all-gather.4.cloned.1.call-start
  7.2 0.7 all-gather.4.cloned.1.call-update
  7.9 0.0 all-gather.6.cloned.1.call-start
  7.9 32.8 %all-gather.4.cloned.1.call-done = bf16[1024,1536]{1,0:T(8,128)(2,1)} async-done(((bf16[256,1536]{1,0:T(8,128)(2,1)}), bf16[1024,1536]{1,0:T(8,128)(2,1)}) %all-gather.4.cloned.1.call-update) | async-done | bytes 3145744 | tf_op jit(solution)/shard_map/all_gather | solution.py:39
  40.8 16.2 %fusion.15 = f32[1024,3072]{1,0:T(8,128)} fusion(bf16[1024,1536]{1,0:T(8,128)(2,1)} %all-gather.4.cloned.1.call-done, bf16[3072,1536]{1,0:T(8,128)(2,1)} %param.5), kind=kOutput, calls=%fused_computation.21 | convolution fusion | flops 9663676416 | bytes 25165824 | tf_op jit(solution)/shard_map/dot_general | solution.py:22
  57.0 0.0 all-gather.6.cloned.1.call-update
  57.0 8.8 copy.5
  65.8 9.9 copy.6
  75.7 5.6 all-to-all-start
  81.3 811.9 %all-gather.6.cloned.1.call-done = f32[4096,3072]{1,0:T(8,128)} async-done(((f32[1024,3072]{1,0:T(8,128)}), f32[4096,3072]{1,0:T(8,128)}) %all-gather.6.cloned.1.call-update) | async-done | bytes 50331664 | tf_op jit(solution)/shard_map/all_gather | solution.py:34
  893.1 23.9 %reduce_sum.11 = f32[1024,3072]{1,0:T(8,128)} reduce(f32[4,1024,3072]{2,1,0:T(8,128)} %bitcast.29, f32[]{:T(128)} %constant.0.clone.1), dimensions={0}, to_apply=%region_0.0 | reduce | flops 9437184 | bytes 62914564 | tf_op jit(solution)/shard_map/reduce_sum | solution.py:34
  917.1 0.0 all-to-all-done
  917.1 13.3 %fusion.7 = bf16[4,256,3072]{2,1,0:T(8,128)(2,1)} fusion(f32[4,256,3072]{2,1,0:T(8,128)} %bitcast.30, bf16[256,4,3072]{2,0,1:T(8,128)(2,1)} %all-to-all-done), kind=kLoop, calls=%fused_computation.10 | loop fusion | flops 62914560 | bytes 25165824 | tf_op jit(solution)/shard_map/convert_element_type | solution.py:35
  930.4 0.0 copy-start
  930.4 5.7 all-to-all-start.1
  936.1 6.1 fusion.12
  942.2 0.0 copy-done
  942.2 12.1 %convolution_convert_fusion = bf16[3072,1536]{1,0:T(8,128)(2,1)} fusion(bf16[1024,3072]{1,0:T(8,128)(2,1)S(1)} %fusion.12, bf16[1024,1536]{1,0:T(8,128)(2,1)S(1)} %copy-done), kind=kOutput, calls=%fused_computation.20 | convolution fusion | flops 9668395008 | bytes 18874368 | tf_op jit(solution)/shard_map/dot_general | solution.py:28
  954.3 52.3 %all-to-all-done.1 = bf16[4,256,3072]{2,1,0:T(8,128)(2,1)} async-done(((bf16[4,256,3072]{2,1,0:T(8,128)(2,1)}), bf16[4,256,3072]{2,1,0:T(8,128)(2,1)}, u32[]{:S(2)}, u32[]{:S(2)}) %all-to-all-start.1) | async-done | bytes 6291488 | tf_op jit(solution)/shard_map/all_to_all | solution.py:43
  1006.6 8.6 copy.7
  1015.2 8.6 copy.8
Async XLA Ops:
  7.2 33.6 %all-gather.4.cloned.1.call-start = ((), (), s32[]{:S(2)}) async-start(), calls=%async_computation.2 | async-start | bytes 3932160 | tf_op jit(solution)/shard_map/all_gather | solution.py:39
  7.9 885.2 %all-gather.6.cloned.1.call-start = ((), (), s32[]{:S(2)}) async-start(), calls=%async_computation.3 | async-start | bytes 62914560 | tf_op jit(solution)/shard_map/all_gather | solution.py:34
  75.7 841.4 %all-to-all-start = ((bf16[256,4,3072]{2,0,1:T(8,128)(2,1)}), bf16[256,4,3072]{2,0,1:T(8,128)(2,1)}, u32[]{:S(2)}, u32[]{:S(2)}) async-start(bf16[256,4,3072]{2,0,1:T(8,128)(2,1)} %copy.6), calls=%async_computation | async-start | bytes 12582912 | tf_op jit(solution)/shard_map/all_to_all | solution.py:40
  930.4 11.8 %copy-start = (bf16[1024,1536]{1,0:T(8,128)(2,1)S(1)}, bf16[1024,1536]{1,0:T(8,128)(2,1)}, u32[]{:S(2)}) copy-start(bf16[1024,1536]{1,0:T(8,128)(2,1)} %all-gather.4.cloned.1.call-done) | copy-start | bytes 9437188
  930.4 76.2 %all-to-all-start.1 = ((bf16[4,256,3072]{2,1,0:T(8,128)(2,1)}), bf16[4,256,3072]{2,1,0:T(8,128)(2,1)}, u32[]{:S(2)}, u32[]{:S(2)}) async-start(bf16[4,256,3072]{2,1,0:T(8,128)(2,1)} %fusion.7), calls=%async_computation.1 | async-start | bytes 12582912 | tf_op jit(solution)/shard_map/all_to_all | solution.py:43
Sparse Core Ops, SparseCore 0:
  9.5 31.2 all-gather.3
  57.1 835.9 all-gather.5
